TPU v7x, 32 devices: a whole 2x2x4 slice. The times are simulated.
32 devices in a mesh: row: 8 (over z, y), col: 4 (over x, core).
Axes of the slice: x: 2, y: 2, z: 4, core: 2. Of those that a mesh axis runs over, the one named last changes fastest.
Arguments:
- root_rhs: bfloat16 [8, 8192], replicated, may hold values from -6 to 6
- diag_inv: bfloat16 [16, 512, 512], replicated, may hold values from -1 to 2
- tile_u: bfloat16 [8, 4, 2, 4, 128, 512], P('row', 'col'), may hold values from -0.1875 to 0.1875
- tile_v: bfloat16 [8, 4, 2, 4, 512, 128], P('row', 'col'), may hold values from -0.25 to 0.25
- tile_rank: int32 [8, 4, 2, 4], P('row', 'col'), may hold values from 16 to 128
- child_x: bfloat16 [32, 8, 512], P(('row', 'col')), may hold values from -6 to 6
- border_t: bfloat16 [32, 512, 1024], P(('row', 'col')), may hold values from -0.09375 to 0.09375
- child_inv: bfloat16 [32, 512, 512], P(('row', 'col')), may hold values from -1 to 2
- child_blocks: int32 [32, 8], P(('row', 'col')), may hold values from 0 to 63
Outputs:
- root_solution: float32 [8, 8192], P(None, ('row', 'col'))
- child_out: float32 [32, 8, 512], P(('row', 'col'))
All inputs are finite; a program needn't handle non-finite values.
Results may differ from a plain program's by a relative error of at most 0.017.
Values sent between devices are 32-bit elements; how exact they have to be, the bound alone decides.
A program may use at most 64 MiB of HBM per device.

v0:
```python
import jax
import jax.numpy as jnp
from jax import lax
from jax.sharding import PartitionSpec as P

BLK = 128
BB = 8


def per_device(
    root_rhs, diag_inv, tile_u, tile_v, tile_rank, child_x, border_t, child_inv, child_blocks
):
    highest_precision = lax.Precision.HIGHEST
    n_row = lax.axis_size("row")
    n_col = lax.axis_size("col")
    my_row = lax.axis_index("row")
    my_col = lax.axis_index("col")
    ntile = diag_inv.shape[0]
    tile = diag_inv.shape[1]
    rhs_count = root_rhs.shape[0]
    rank_max = tile_u.shape[4]
    t_rows = tile_u.shape[2]
    t_cols = tile_u.shape[3]
    left_tiles = tile_u[0, 0]
    right_tiles = tile_v[0, 0]
    tile_ranks = tile_rank[0, 0]
    blocks_per_front = tile // BLK
    n_child = child_x.shape[0]
    upward = jnp.einsum("crs,csb->crb", child_x, border_t, preferred_element_type=jnp.float32)
    pieces = (
        upward.reshape(n_child, rhs_count, BB, BLK)
        .transpose(1, 0, 2, 3)
        .reshape(rhs_count, n_child * BB, BLK)
    )
    flat_blocks = child_blocks.reshape(-1)
    dense_sum = (
        jnp.zeros((rhs_count, ntile * blocks_per_front, BLK), jnp.float32)
        .at[:, flat_blocks, :]
        .add(pieces)
    )
    dense_sum = dense_sum.reshape(rhs_count, ntile, tile)
    right_side = root_rhs.reshape(rhs_count, ntile, tile)
    col_ids = my_col + n_col * jnp.arange(t_cols)
    row_ids = my_row + n_row * jnp.arange(t_rows)
    rank_iota = jnp.arange(rank_max)

    def forward(column, solved_rows):
        owner_slot = column // n_row
        on_row = column % n_row == my_row
        known_cols = jnp.take(solved_rows, col_ids, axis=1).astype(jnp.bfloat16)
        right_row = lax.dynamic_index_in_dim(right_tiles, owner_slot, 0, keepdims=False)
        left_row_index = lax.dynamic_index_in_dim(left_tiles, owner_slot, 0, keepdims=False)
        rank_row = lax.dynamic_index_in_dim(tile_ranks, owner_slot, 0, keepdims=False)
        live_mask = (rank_iota[None, :] < rank_row[:, None]) & (col_ids[:, None] < column) & on_row
        coefficient_values = jnp.einsum(
            "rbt,btq->rbq", known_cols, right_row, preferred_element_type=jnp.float32
        )
        coefficient_values = jnp.where(live_mask[None], coefficient_values, 0.0).astype(
            jnp.bfloat16
        )
        partial_value = jnp.einsum(
            "rbq,bqt->rt", coefficient_values, left_row_index, preferred_element_type=jnp.float32
        )
        carried = lax.dynamic_index_in_dim(dense_sum, column, 1, keepdims=False)
        row_total = lax.psum(partial_value + carried, ("row", "col"))
        block_rhs = lax.dynamic_index_in_dim(right_side, column, 1, keepdims=False).astype(
            jnp.float32
        )
        inverse = lax.dynamic_index_in_dim(diag_inv, column, 0, keepdims=False).astype(jnp.float32)
        fresh = jnp.dot(block_rhs - row_total, inverse, precision=highest_precision)
        return lax.dynamic_update_index_in_dim(solved_rows, fresh, column, 1)

    solved_rows = lax.fori_loop(0, ntile, forward, jnp.zeros((rhs_count, ntile, tile), jnp.float32))

    def backward(sweep, result):
        column = ntile - 1 - sweep
        owner_slot = column // n_col
        on_col = column % n_col == my_col
        known_rows = jnp.take(result, row_ids, axis=1).astype(jnp.bfloat16)
        left_col = lax.dynamic_index_in_dim(left_tiles, owner_slot, 1, keepdims=False)
        right_col = lax.dynamic_index_in_dim(right_tiles, owner_slot, 1, keepdims=False)
        rank_col = lax.dynamic_index_in_dim(tile_ranks, owner_slot, 1, keepdims=False)
        live_mask = (rank_iota[None, :] < rank_col[:, None]) & (row_ids[:, None] > column) & on_col
        coefficient_values = jnp.einsum(
            "rat,aqt->raq", known_rows, left_col, preferred_element_type=jnp.float32
        )
        coefficient_values = jnp.where(live_mask[None], coefficient_values, 0.0).astype(
            jnp.bfloat16
        )
        partial_value = jnp.einsum(
            "raq,atq->rt", coefficient_values, right_col, preferred_element_type=jnp.float32
        )
        col_total = lax.psum(partial_value, ("row", "col"))
        block_solved = lax.dynamic_index_in_dim(solved_rows, column, 1, keepdims=False)
        inverse = lax.dynamic_index_in_dim(diag_inv, column, 0, keepdims=False).astype(jnp.float32)
        fresh = jnp.dot(block_solved - col_total, inverse.T, precision=highest_precision)
        return lax.dynamic_update_index_in_dim(result, fresh, column, 1)

    result = lax.fori_loop(0, ntile, backward, jnp.zeros((rhs_count, ntile, tile), jnp.float32))
    share = ntile * tile // (n_row * n_col)
    start = (my_row * n_col + my_col) * share
    root_part = lax.dynamic_slice_in_dim(result.reshape(rhs_count, ntile * tile), start, share, 1)
    gathered = result.reshape(rhs_count, ntile * blocks_per_front, BLK)[:, flat_blocks, :]
    gathered = gathered.reshape(rhs_count, n_child, BB * BLK).astype(jnp.bfloat16)
    returned = jnp.einsum("rcb,csb->crs", gathered, border_t, preferred_element_type=jnp.float32)
    child_out = child_x.astype(jnp.float32) - jnp.einsum(
        "crs,cst->crt", returned, child_inv.astype(jnp.float32), precision=highest_precision
    )
    return (root_part, child_out)


def solution(mesh):
    return jax.shard_map(
        per_device,
        mesh=mesh,
        in_specs=(
            P(),
            P(),
            P("row", "col", None, None, None, None),
            P("row", "col", None, None, None, None),
            P("row", "col", None, None),
            P(("row", "col"), None, None),
            P(("row", "col"), None, None),
            P(("row", "col"), None, None),
            P(("row", "col"), None),
        ),
        out_specs=(P(None, ("row", "col")), P(("row", "col"), None, None)),
        check_vma=False,
    )
```

profile of v0, /device:TPU:0, one launch (start us, length us, event | category | flops | bytes accessed | tf_op | source)
XLA Modules:
  0.0 1424.4 jit_solution(4886888711580385367)
XLA Ops:
  5.8 715.2 %while.32 = (s32[]{:T(128)}, f32[8,16,512]{2,0,1:T(8,128)S(1)}, bf16[8,16,512]{2,1,0:T(8,128)(2,1)S(1)}, s32[2,4]{1,0:T(2,128)}, s32[]{:T(128)}, /*index=5*/bf16...) while((s32[]{:T(128)}, f32[8,16,512]{2,0,1:T(8,128)S(1)}, ...), condition=%wide.region_3.4_spmd.clone, body=%wide.region_1.3_spmd.clone.sunk | while | flops 33598024 | bytes 1818560 | solution.py:73
  9.0 42.0 %psum.32 = f32[8,512]{1,0:T(8,128)S(1)} all-reduce(f32[8,512]{1,0:T(8,128)S(1)} %fusion.106), channel_id=1, replica_groups=mesh['row'=8,'col'=4] {'row','col'}, use_global_device_ids=true, to_apply=%region_2.2 | all-reduce | flops 4096 | bytes 32768 | tf_op jit(solution)/shard_map/while/body/eval_jaxpr/psum | solution.py:65
  55.5 40.2 %psum.32 = f32[8,512]{1,0:T(8,128)S(1)} all-reduce(f32[8,512]{1,0:T(8,128)S(1)} %fusion.106), channel_id=1, replica_groups=mesh['row'=8,'col'=4] {'row','col'}, use_global_device_ids=true, to_apply=%region_2.2 | all-reduce | flops 4096 | bytes 32768 | tf_op jit(solution)/shard_map/while/body/eval_jaxpr/psum | solution.py:65
  100.2 40.0 %psum.32 = f32[8,512]{1,0:T(8,128)S(1)} all-reduce(f32[8,512]{1,0:T(8,128)S(1)} %fusion.106), channel_id=1, replica_groups=mesh['row'=8,'col'=4] {'row','col'}, use_global_device_ids=true, to_apply=%region_2.2 | all-reduce | flops 4096 | bytes 32768 | tf_op jit(solution)/shard_map/while/body/eval_jaxpr/psum | solution.py:65
  144.7 40.2 %psum.32 = f32[8,512]{1,0:T(8,128)S(1)} all-reduce(f32[8,512]{1,0:T(8,128)S(1)} %fusion.106), channel_id=1, replica_groups=mesh['row'=8,'col'=4] {'row','col'}, use_global_device_ids=true, to_apply=%region_2.2 | all-reduce | flops 4096 | bytes 32768 | tf_op jit(solution)/shard_map/while/body/eval_jaxpr/psum | solution.py:65
  189.4 39.9 %psum.32 = f32[8,512]{1,0:T(8,128)S(1)} all-reduce(f32[8,512]{1,0:T(8,128)S(1)} %fusion.106), channel_id=1, replica_groups=mesh['row'=8,'col'=4] {'row','col'}, use_global_device_ids=true, to_apply=%region_2.2 | all-reduce | flops 4096 | bytes 32768 | tf_op jit(solution)/shard_map/while/body/eval_jaxpr/psum | solution.py:65
  233.8 40.1 %psum.32 = f32[8,512]{1,0:T(8,128)S(1)} all-reduce(f32[8,512]{1,0:T(8,128)S(1)} %fusion.106), channel_id=1, replica_groups=mesh['row'=8,'col'=4] {'row','col'}, use_global_device_ids=true, to_apply=%region_2.2 | all-reduce | flops 4096 | bytes 32768 | tf_op jit(solution)/shard_map/while/body/eval_jaxpr/psum | solution.py:65
  278.5 40.0 %psum.32 = f32[8,512]{1,0:T(8,128)S(1)} all-reduce(f32[8,512]{1,0:T(8,128)S(1)} %fusion.106), channel_id=1, replica_groups=mesh['row'=8,'col'=4] {'row','col'}, use_global_device_ids=true, to_apply=%region_2.2 | all-reduce | flops 4096 | bytes 32768 | tf_op jit(solution)/shard_map/while/body/eval_jaxpr/psum | solution.py:65
  323.0 40.2 %psum.32 = f32[8,512]{1,0:T(8,128)S(1)} all-reduce(f32[8,512]{1,0:T(8,128)S(1)} %fusion.106), channel_id=1, replica_groups=mesh['row'=8,'col'=4] {'row','col'}, use_global_device_ids=true, to_apply=%region_2.2 | all-reduce | flops 4096 | bytes 32768 | tf_op jit(solution)/shard_map/while/body/eval_jaxpr/psum | solution.py:65
  367.7 39.8 %psum.32 = f32[8,512]{1,0:T(8,128)S(1)} all-reduce(f32[8,512]{1,0:T(8,128)S(1)} %fusion.106), channel_id=1, replica_groups=mesh['row'=8,'col'=4] {'row','col'}, use_global_device_ids=true, to_apply=%region_2.2 | all-reduce | flops 4096 | bytes 32768 | tf_op jit(solution)/shard_map/while/body/eval_jaxpr/psum | solution.py:65
  412.0 40.2 %psum.32 = f32[8,512]{1,0:T(8,128)S(1)} all-reduce(f32[8,512]{1,0:T(8,128)S(1)} %fusion.106), channel_id=1, replica_groups=mesh['row'=8,'col'=4] {'row','col'}, use_global_device_ids=true, to_apply=%region_2.2 | all-reduce | flops 4096 | bytes 32768 | tf_op jit(solution)/shard_map/while/body/eval_jaxpr/psum | solution.py:65
  456.7 39.8 %psum.32 = f32[8,512]{1,0:T(8,128)S(1)} all-reduce(f32[8,512]{1,0:T(8,128)S(1)} %fusion.106), channel_id=1, replica_groups=mesh['row'=8,'col'=4] {'row','col'}, use_global_device_ids=true, to_apply=%region_2.2 | all-reduce | flops 4096 | bytes 32768 | tf_op jit(solution)/shard_map/while/body/eval_jaxpr/psum | solution.py:65
  501.1 40.2 %psum.32 = f32[8,512]{1,0:T(8,128)S(1)} all-reduce(f32[8,512]{1,0:T(8,128)S(1)} %fusion.106), channel_id=1, replica_groups=mesh['row'=8,'col'=4] {'row','col'}, use_global_device_ids=true, to_apply=%region_2.2 | all-reduce | flops 4096 | bytes 32768 | tf_op jit(solution)/shard_map/while/body/eval_jaxpr/psum | solution.py:65
  545.8 39.8 %psum.32 = f32[8,512]{1,0:T(8,128)S(1)} all-reduce(f32[8,512]{1,0:T(8,128)S(1)} %fusion.106), channel_id=1, replica_groups=mesh['row'=8,'col'=4] {'row','col'}, use_global_device_ids=true, to_apply=%region_2.2 | all-reduce | flops 4096 | bytes 32768 | tf_op jit(solution)/shard_map/while/body/eval_jaxpr/psum | solution.py:65
  590.1 40.3 %psum.32 = f32[8,512]{1,0:T(8,128)S(1)} all-reduce(f32[8,512]{1,0:T(8,128)S(1)} %fusion.106), channel_id=1, replica_groups=mesh['row'=8,'col'=4] {'row','col'}, use_global_device_ids=true, to_apply=%region_2.2 | all-reduce | flops 4096 | bytes 32768 | tf_op jit(solution)/shard_map/while/body/eval_jaxpr/psum | solution.py:65
  635.0 39.7 %psum.32 = f32[8,512]{1,0:T(8,128)S(1)} all-reduce(f32[8,512]{1,0:T(8,128)S(1)} %fusion.106), channel_id=1, replica_groups=mesh['row'=8,'col'=4] {'row','col'}, use_global_device_ids=true, to_apply=%region_2.2 | all-reduce | flops 4096 | bytes 32768 | tf_op jit(solution)/shard_map/while/body/eval_jaxpr/psum | solution.py:65
  679.2 40.4 %psum.32 = f32[8,512]{1,0:T(8,128)S(1)} all-reduce(f32[8,512]{1,0:T(8,128)S(1)} %fusion.106), channel_id=1, replica_groups=mesh['row'=8,'col'=4] {'row','col'}, use_global_device_ids=true, to_apply=%region_2.2 | all-reduce | flops 4096 | bytes 32768 | tf_op jit(solution)/shard_map/while/body/eval_jaxpr/psum | solution.py:65
  721.8 700.1 %while.33 = (s32[]{:T(128)}, f32[8,16,512]{2,0,1:T(8,128)S(1)}, f32[8,16,512]{2,0,1:T(8,128)S(1)}, s32[2,4]{0,1:T(4,128)S(1)}, s32[]{:T(128)}, /*index=5*/bf16[2...) while((s32[]{:T(128)}, f32[8,16,512]{2,0,1:T(8,128)S(1)}, ...), condition=%wide.region_6.7_spmd.clone, body=%wide.region_4.6_spmd.clone.sunk | while | flops 29382456 | bytes 1203697 | solution.py:99
  724.0 39.6 %psum.33 = f32[8,512]{1,0:T(8,128)S(1)} all-reduce(f32[8,512]{1,0:T(8,128)S(1)} %fusion.113), channel_id=1, replica_groups=mesh['row'=8,'col'=4] {'row','col'}, use_global_device_ids=true, to_apply=%region_5.5 | all-reduce | flops 4096 | bytes 32768 | tf_op jit(solution)/shard_map/while/body/eval_jaxpr/psum | solution.py:93
  767.2 40.5 %psum.33 = f32[8,512]{1,0:T(8,128)S(1)} all-reduce(f32[8,512]{1,0:T(8,128)S(1)} %fusion.113), channel_id=1, replica_groups=mesh['row'=8,'col'=4] {'row','col'}, use_global_device_ids=true, to_apply=%region_5.5 | all-reduce | flops 4096 | bytes 32768 | tf_op jit(solution)/shard_map/while/body/eval_jaxpr/psum | solution.py:93
  811.5 39.5 %psum.33 = f32[8,512]{1,0:T(8,128)S(1)} all-reduce(f32[8,512]{1,0:T(8,128)S(1)} %fusion.113), channel_id=1, replica_groups=mesh['row'=8,'col'=4] {'row','col'}, use_global_device_ids=true, to_apply=%region_5.5 | all-reduce | flops 4096 | bytes 32768 | tf_op jit(solution)/shard_map/while/body/eval_jaxpr/psum | solution.py:93
  854.7 40.6 %psum.33 = f32[8,512]{1,0:T(8,128)S(1)} all-reduce(f32[8,512]{1,0:T(8,128)S(1)} %fusion.113), channel_id=1, replica_groups=mesh['row'=8,'col'=4] {'row','col'}, use_global_device_ids=true, to_apply=%region_5.5 | all-reduce | flops 4096 | bytes 32768 | tf_op jit(solution)/shard_map/while/body/eval_jaxpr/psum | solution.py:93
  899.0 39.4 %psum.33 = f32[8,512]{1,0:T(8,128)S(1)} all-reduce(f32[8,512]{1,0:T(8,128)S(1)} %fusion.113), channel_id=1, replica_groups=mesh['row'=8,'col'=4] {'row','col'}, use_global_device_ids=true, to_apply=%region_5.5 | all-reduce | flops 4096 | bytes 32768 | tf_op jit(solution)/shard_map/while/body/eval_jaxpr/psum | solution.py:93
  942.1 40.7 %psum.33 = f32[8,512]{1,0:T(8,128)S(1)} all-reduce(f32[8,512]{1,0:T(8,128)S(1)} %fusion.113), channel_id=1, replica_groups=mesh['row'=8,'col'=4] {'row','col'}, use_global_device_ids=true, to_apply=%region_5.5 | all-reduce | flops 4096 | bytes 32768 | tf_op jit(solution)/shard_map/while/body/eval_jaxpr/psum | solution.py:93
  986.5 39.4 %psum.33 = f32[8,512]{1,0:T(8,128)S(1)} all-reduce(f32[8,512]{1,0:T(8,128)S(1)} %fusion.113), channel_id=1, replica_groups=mesh['row'=8,'col'=4] {'row','col'}, use_global_device_ids=true, to_apply=%region_5.5 | all-reduce | flops 4096 | bytes 32768 | tf_op jit(solution)/shard_map/while/body/eval_jaxpr/psum | solution.py:93
  1029.6 40.7 %psum.33 = f32[8,512]{1,0:T(8,128)S(1)} all-reduce(f32[8,512]{1,0:T(8,128)S(1)} %fusion.113), channel_id=1, replica_groups=mesh['row'=8,'col'=4] {'row','col'}, use_global_device_ids=true, to_apply=%region_5.5 | all-reduce | flops 4096 | bytes 32768 | tf_op jit(solution)/shard_map/while/body/eval_jaxpr/psum | solution.py:93
  1074.0 39.4 %psum.33 = f32[8,512]{1,0:T(8,128)S(1)} all-reduce(f32[8,512]{1,0:T(8,128)S(1)} %fusion.113), channel_id=1, replica_groups=mesh['row'=8,'col'=4] {'row','col'}, use_global_device_ids=true, to_apply=%region_5.5 | all-reduce | flops 4096 | bytes 32768 | tf_op jit(solution)/shard_map/while/body/eval_jaxpr/psum | solution.py:93
  1117.1 40.7 %psum.33 = f32[8,512]{1,0:T(8,128)S(1)} all-reduce(f32[8,512]{1,0:T(8,128)S(1)} %fusion.113), channel_id=1, replica_groups=mesh['row'=8,'col'=4] {'row','col'}, use_global_device_ids=true, to_apply=%region_5.5 | all-reduce | flops 4096 | bytes 32768 | tf_op jit(solution)/shard_map/while/body/eval_jaxpr/psum | solution.py:93
  1204.6 40.7 %psum.33 = f32[8,512]{1,0:T(8,128)S(1)} all-reduce(f32[8,512]{1,0:T(8,128)S(1)} %fusion.113), channel_id=1, replica_groups=mesh['row'=8,'col'=4] {'row','col'}, use_global_device_ids=true, to_apply=%region_5.5 | all-reduce | flops 4096 | bytes 32768 | tf_op jit(solution)/shard_map/while/body/eval_jaxpr/psum | solution.py:93
  1292.2 40.7 %psum.33 = f32[8,512]{1,0:T(8,128)S(1)} all-reduce(f32[8,512]{1,0:T(8,128)S(1)} %fusion.113), channel_id=1, replica_groups=mesh['row'=8,'col'=4] {'row','col'}, use_global_device_ids=true, to_apply=%region_5.5 | all-reduce | flops 4096 | bytes 32768 | tf_op jit(solution)/shard_map/while/body/eval_jaxpr/psum | solution.py:93
  1336.5 39.4 %psum.33 = f32[8,512]{1,0:T(8,128)S(1)} all-reduce(f32[8,512]{1,0:T(8,128)S(1)} %fusion.113), channel_id=1, replica_groups=mesh['row'=8,'col'=4] {'row','col'}, use_global_device_ids=true, to_apply=%region_5.5 | all-reduce | flops 4096 | bytes 32768 | tf_op jit(solution)/shard_map/while/body/eval_jaxpr/psum | solution.py:93
  1379.7 40.7 %psum.33 = f32[8,512]{1,0:T(8,128)S(1)} all-reduce(f32[8,512]{1,0:T(8,128)S(1)} %fusion.113), channel_id=1, replica_groups=mesh['row'=8,'col'=4] {'row','col'}, use_global_device_ids=true, to_apply=%region_5.5 | all-reduce | flops 4096 | bytes 32768 | tf_op jit(solution)/shard_map/while/body/eval_jaxpr/psum | solution.py:93
  (278 shorter events, 217.6 us)
Async XLA Ops:
  0.6 1422.8 %copy-start = (bf16[1,512,512]{2,1,0:T(8,128)(2,1)S(1)}, bf16[1,512,512]{2,1,0:T(8,128)(2,1)}, u32[]{:S(2)}) copy-start(bf16[1,512,512]{2,1,0:T(8,128)(2,1)} %param.20) | copy-start | bytes 1572868
  5.7 1417.3 %copy-start.1 = (bf16[1,512,1024]{2,1,0:T(8,128)(2,1)S(1)}, bf16[1,512,1024]{2,1,0:T(8,128)(2,1)}, u32[]{:S(2)}) copy-start(bf16[1,512,1024]{2,1,0:T(8,128)(2,1)} %param.19) | copy-start | bytes 3145732
  5.8 1417.7 %copy-start.2 = (bf16[1,8,512]{2,1,0:T(8,128)(2,1)S(1)}, bf16[1,8,512]{2,1,0:T(8,128)(2,1)}, u32[]{:S(2)}) copy-start(bf16[1,8,512]{2,1,0:T(8,128)(2,1)} %param.18) | copy-start | bytes 24580
where the time goes:
time: 1430 us; the launch traced here: 1420 us
  blocking collectives  1280 us (90%)
  matrix products  100 us (7%)
  local copies, waits for them, and re-layouts  33.4 us (2%)
    psum x16, blocking collectives, forward(): row_total = lax.psum(partial_value + carried, ('row', 'col'))  643 us
    psum x16, blocking collectives, backward(): col_total = lax.psum(partial_value, ('row', 'col'))  641 us

commit v1 on v0

--- a/solution.py
+++ b/solution.py
@@ -5,6 +5,11 @@
 
 BLK = 128
 BB = 8
+
+
+def gather_and_add(value, axis):
+    parts = lax.all_gather(value, axis)
+    return jnp.sum(parts, axis=0)
 
 
 def per_device(
@@ -90,7 +95,7 @@
         partial_value = jnp.einsum(
             "raq,atq->rt", coefficient_values, right_col, preferred_element_type=jnp.float32
         )
-        col_total = lax.psum(partial_value, ("row", "col"))
+        col_total = gather_and_add(partial_value, ("row", "col"))
         block_solved = lax.dynamic_index_in_dim(solved_rows, column, 1, keepdims=False)
         inverse = lax.dynamic_index_in_dim(diag_inv, column, 0, keepdims=False).astype(jnp.float32)
         fresh = jnp.dot(block_solved - col_total, inverse.T, precision=highest_precision)

time: 1430 us -> 1410 us (0.986)
    psum x16 -> x0, blocking collectives: 641 us -> none  [backward(): col_total = lax.psum(partial_value, ('row', 'col'))]
    all_gather x0 -> x16, blocking collectives: none -> 623 us  [gather_and_add(): parts = lax.all_gather(value, axis)]
where the time goes in v1:
time: 1410 us
  blocking collectives  1270 us (90%)
  matrix products  97.7 us (7%)
  local copies, waits for them, and re-layouts  34.8 us (2%)
    psum x16, blocking collectives, forward(): row_total = lax.psum(partial_value + carried, ('row', 'col'))  643 us
    all_gather x16, blocking collectives, gather_and_add(): parts = lax.all_gather(value, axis)  623 us
    dot_general x16, matrix products, forward(): jnp.einsum('rbq,bqt->rt', coefficient_values, left_row_index, preferred_e...  28.5 us

profile of v1, /device:TPU:0, one launch (start us, length us, event | category | flops | bytes accessed | tf_op | source)
XLA Modules:
  0.0 1406.6 jit_solution(297303613746316633)
XLA Ops:
  5.7 715.3 %while.32 = (s32[]{:T(128)}, f32[8,16,512]{2,0,1:T(8,128)S(1)}, bf16[8,16,512]{2,1,0:T(8,128)(2,1)S(1)}, s32[2,4]{1,0:T(2,128)}, s32[]{:T(128)}, /*index=5*/bf16...) while((s32[]{:T(128)}, f32[8,16,512]{2,0,1:T(8,128)S(1)}, ...), condition=%wide.region_3.4_spmd.clone, body=%wide.region_1.3_spmd.clone.sunk | while | flops 33598024 | bytes 1818560 | solution.py:78
  8.9 42.0 %psum.16 = f32[8,512]{1,0:T(8,128)S(1)} all-reduce(f32[8,512]{1,0:T(8,128)S(1)} %fusion.105), channel_id=1, replica_groups=mesh['row'=8,'col'=4] {'row','col'}, use_global_device_ids=true, to_apply=%region_2.2 | all-reduce | flops 4096 | bytes 32768 | tf_op jit(solution)/shard_map/while/body/eval_jaxpr/psum | solution.py:70
  55.4 40.2 %psum.16 = f32[8,512]{1,0:T(8,128)S(1)} all-reduce(f32[8,512]{1,0:T(8,128)S(1)} %fusion.105), channel_id=1, replica_groups=mesh['row'=8,'col'=4] {'row','col'}, use_global_device_ids=true, to_apply=%region_2.2 | all-reduce | flops 4096 | bytes 32768 | tf_op jit(solution)/shard_map/while/body/eval_jaxpr/psum | solution.py:70
  100.1 40.0 %psum.16 = f32[8,512]{1,0:T(8,128)S(1)} all-reduce(f32[8,512]{1,0:T(8,128)S(1)} %fusion.105), channel_id=1, replica_groups=mesh['row'=8,'col'=4] {'row','col'}, use_global_device_ids=true, to_apply=%region_2.2 | all-reduce | flops 4096 | bytes 32768 | tf_op jit(solution)/shard_map/while/body/eval_jaxpr/psum | solution.py:70
  144.6 40.2 %psum.16 = f32[8,512]{1,0:T(8,128)S(1)} all-reduce(f32[8,512]{1,0:T(8,128)S(1)} %fusion.105), channel_id=1, replica_groups=mesh['row'=8,'col'=4] {'row','col'}, use_global_device_ids=true, to_apply=%region_2.2 | all-reduce | flops 4096 | bytes 32768 | tf_op jit(solution)/shard_map/while/body/eval_jaxpr/psum | solution.py:70
  189.3 39.9 %psum.16 = f32[8,512]{1,0:T(8,128)S(1)} all-reduce(f32[8,512]{1,0:T(8,128)S(1)} %fusion.105), channel_id=1, replica_groups=mesh['row'=8,'col'=4] {'row','col'}, use_global_device_ids=true, to_apply=%region_2.2 | all-reduce | flops 4096 | bytes 32768 | tf_op jit(solution)/shard_map/while/body/eval_jaxpr/psum | solution.py:70
  233.7 40.1 %psum.16 = f32[8,512]{1,0:T(8,128)S(1)} all-reduce(f32[8,512]{1,0:T(8,128)S(1)} %fusion.105), channel_id=1, replica_groups=mesh['row'=8,'col'=4] {'row','col'}, use_global_device_ids=true, to_apply=%region_2.2 | all-reduce | flops 4096 | bytes 32768 | tf_op jit(solution)/shard_map/while/body/eval_jaxpr/psum | solution.py:70
  278.4 39.9 %psum.16 = f32[8,512]{1,0:T(8,128)S(1)} all-reduce(f32[8,512]{1,0:T(8,128)S(1)} %fusion.105), channel_id=1, replica_groups=mesh['row'=8,'col'=4] {'row','col'}, use_global_device_ids=true, to_apply=%region_2.2 | all-reduce | flops 4096 | bytes 32768 | tf_op jit(solution)/shard_map/while/body/eval_jaxpr/psum | solution.py:70
  322.8 40.2 %psum.16 = f32[8,512]{1,0:T(8,128)S(1)} all-reduce(f32[8,512]{1,0:T(8,128)S(1)} %fusion.105), channel_id=1, replica_groups=mesh['row'=8,'col'=4] {'row','col'}, use_global_device_ids=true, to_apply=%region_2.2 | all-reduce | flops 4096 | bytes 32768 | tf_op jit(solution)/shard_map/while/body/eval_jaxpr/psum | solution.py:70
  367.6 39.8 %psum.16 = f32[8,512]{1,0:T(8,128)S(1)} all-reduce(f32[8,512]{1,0:T(8,128)S(1)} %fusion.105), channel_id=1, replica_groups=mesh['row'=8,'col'=4] {'row','col'}, use_global_device_ids=true, to_apply=%region_2.2 | all-reduce | flops 4096 | bytes 32768 | tf_op jit(solution)/shard_map/while/body/eval_jaxpr/psum | solution.py:70
  411.9 40.2 %psum.16 = f32[8,512]{1,0:T(8,128)S(1)} all-reduce(f32[8,512]{1,0:T(8,128)S(1)} %fusion.105), channel_id=1, replica_groups=mesh['row'=8,'col'=4] {'row','col'}, use_global_device_ids=true, to_apply=%region_2.2 | all-reduce | flops 4096 | bytes 32768 | tf_op jit(solution)/shard_map/while/body/eval_jaxpr/psum | solution.py:70
  456.7 39.8 %psum.16 = f32[8,512]{1,0:T(8,128)S(1)} all-reduce(f32[8,512]{1,0:T(8,128)S(1)} %fusion.105), channel_id=1, replica_groups=mesh['row'=8,'col'=4] {'row','col'}, use_global_device_ids=true, to_apply=%region_2.2 | all-reduce | flops 4096 | bytes 32768 | tf_op jit(solution)/shard_map/while/body/eval_jaxpr/psum | solution.py:70
  501.0 40.4 %psum.16 = f32[8,512]{1,0:T(8,128)S(1)} all-reduce(f32[8,512]{1,0:T(8,128)S(1)} %fusion.105), channel_id=1, replica_groups=mesh['row'=8,'col'=4] {'row','col'}, use_global_device_ids=true, to_apply=%region_2.2 | all-reduce | flops 4096 | bytes 32768 | tf_op jit(solution)/shard_map/while/body/eval_jaxpr/psum | solution.py:70
  545.9 39.7 %psum.16 = f32[8,512]{1,0:T(8,128)S(1)} all-reduce(f32[8,512]{1,0:T(8,128)S(1)} %fusion.105), channel_id=1, replica_groups=mesh['row'=8,'col'=4] {'row','col'}, use_global_device_ids=true, to_apply=%region_2.2 | all-reduce | flops 4096 | bytes 32768 | tf_op jit(solution)/shard_map/while/body/eval_jaxpr/psum | solution.py:70
  590.0 40.4 %psum.16 = f32[8,512]{1,0:T(8,128)S(1)} all-reduce(f32[8,512]{1,0:T(8,128)S(1)} %fusion.105), channel_id=1, replica_groups=mesh['row'=8,'col'=4] {'row','col'}, use_global_device_ids=true, to_apply=%region_2.2 | all-reduce | flops 4096 | bytes 32768 | tf_op jit(solution)/shard_map/while/body/eval_jaxpr/psum | solution.py:70
  635.0 39.6 %psum.16 = f32[8,512]{1,0:T(8,128)S(1)} all-reduce(f32[8,512]{1,0:T(8,128)S(1)} %fusion.105), channel_id=1, replica_groups=mesh['row'=8,'col'=4] {'row','col'}, use_global_device_ids=true, to_apply=%region_2.2 | all-reduce | flops 4096 | bytes 32768 | tf_op jit(solution)/shard_map/while/body/eval_jaxpr/psum | solution.py:70
  679.1 40.5 %psum.16 = f32[8,512]{1,0:T(8,128)S(1)} all-reduce(f32[8,512]{1,0:T(8,128)S(1)} %fusion.105), channel_id=1, replica_groups=mesh['row'=8,'col'=4] {'row','col'}, use_global_device_ids=true, to_apply=%region_2.2 | all-reduce | flops 4096 | bytes 32768 | tf_op jit(solution)/shard_map/while/body/eval_jaxpr/psum | solution.py:70
  723.2 680.9 %while.33 = (s32[]{:T(128)}, f32[8,16,512]{2,0,1:T(8,128)S(1)}, f32[8,16,512]{2,0,1:T(8,128)S(1)}, s32[2,4]{0,1:T(4,128)S(1)}, s32[]{:T(128)}, /*index=5*/bf16[2...) while((s32[]{:T(128)}, f32[8,16,512]{2,0,1:T(8,128)S(1)}, ...), condition=%wide.region_6.7_spmd.clone, body=%wide.region_4.6_spmd.clone.sunk | while | flops 29505336 | bytes 2318067 | solution.py:104
  725.2 42.6 %all-gather.3 = f32[256,512]{1,0:T(8,128)S(1)} all-gather(f32[8,512]{1,0:T(8,128)S(1)} %convolution_bitcast_fusion.6), channel_id=2, replica_groups=mesh['row'=8,'col'=4] {'row','col'}, dimensions={0}, use_global_device_ids=true | all-gather | bytes 540672 | tf_op jit(solution)/shard_map/while/body/eval_jaxpr/all_gather | solution.py:11
  771.4 38.1 %all-gather.3 = f32[256,512]{1,0:T(8,128)S(1)} all-gather(f32[8,512]{1,0:T(8,128)S(1)} %convolution_bitcast_fusion.6), channel_id=2, replica_groups=mesh['row'=8,'col'=4] {'row','col'}, dimensions={0}, use_global_device_ids=true | all-gather | bytes 540672 | tf_op jit(solution)/shard_map/while/body/eval_jaxpr/all_gather | solution.py:11
  813.0 39.4 %all-gather.3 = f32[256,512]{1,0:T(8,128)S(1)} all-gather(f32[8,512]{1,0:T(8,128)S(1)} %convolution_bitcast_fusion.6), channel_id=2, replica_groups=mesh['row'=8,'col'=4] {'row','col'}, dimensions={0}, use_global_device_ids=true | all-gather | bytes 540672 | tf_op jit(solution)/shard_map/while/body/eval_jaxpr/all_gather | solution.py:11
  856.1 38.1 %all-gather.3 = f32[256,512]{1,0:T(8,128)S(1)} all-gather(f32[8,512]{1,0:T(8,128)S(1)} %convolution_bitcast_fusion.6), channel_id=2, replica_groups=mesh['row'=8,'col'=4] {'row','col'}, dimensions={0}, use_global_device_ids=true | all-gather | bytes 540672 | tf_op jit(solution)/shard_map/while/body/eval_jaxpr/all_gather | solution.py:11
  897.8 39.4 %all-gather.3 = f32[256,512]{1,0:T(8,128)S(1)} all-gather(f32[8,512]{1,0:T(8,128)S(1)} %convolution_bitcast_fusion.6), channel_id=2, replica_groups=mesh['row'=8,'col'=4] {'row','col'}, dimensions={0}, use_global_device_ids=true | all-gather | bytes 540672 | tf_op jit(solution)/shard_map/while/body/eval_jaxpr/all_gather | solution.py:11
  940.8 38.1 %all-gather.3 = f32[256,512]{1,0:T(8,128)S(1)} all-gather(f32[8,512]{1,0:T(8,128)S(1)} %convolution_bitcast_fusion.6), channel_id=2, replica_groups=mesh['row'=8,'col'=4] {'row','col'}, dimensions={0}, use_global_device_ids=true | all-gather | bytes 540672 | tf_op jit(solution)/shard_map/while/body/eval_jaxpr/all_gather | solution.py:11
  982.5 39.4 %all-gather.3 = f32[256,512]{1,0:T(8,128)S(1)} all-gather(f32[8,512]{1,0:T(8,128)S(1)} %convolution_bitcast_fusion.6), channel_id=2, replica_groups=mesh['row'=8,'col'=4] {'row','col'}, dimensions={0}, use_global_device_ids=true | all-gather | bytes 540672 | tf_op jit(solution)/shard_map/while/body/eval_jaxpr/all_gather | solution.py:11
  1025.5 38.1 %all-gather.3 = f32[256,512]{1,0:T(8,128)S(1)} all-gather(f32[8,512]{1,0:T(8,128)S(1)} %convolution_bitcast_fusion.6), channel_id=2, replica_groups=mesh['row'=8,'col'=4] {'row','col'}, dimensions={0}, use_global_device_ids=true | all-gather | bytes 540672 | tf_op jit(solution)/shard_map/while/body/eval_jaxpr/all_gather | solution.py:11
  1067.2 39.4 %all-gather.3 = f32[256,512]{1,0:T(8,128)S(1)} all-gather(f32[8,512]{1,0:T(8,128)S(1)} %convolution_bitcast_fusion.6), channel_id=2, replica_groups=mesh['row'=8,'col'=4] {'row','col'}, dimensions={0}, use_global_device_ids=true | all-gather | bytes 540672 | tf_op jit(solution)/shard_map/while/body/eval_jaxpr/all_gather | solution.py:11
  1110.2 38.1 %all-gather.3 = f32[256,512]{1,0:T(8,128)S(1)} all-gather(f32[8,512]{1,0:T(8,128)S(1)} %convolution_bitcast_fusion.6), channel_id=2, replica_groups=mesh['row'=8,'col'=4] {'row','col'}, dimensions={0}, use_global_device_ids=true | all-gather | bytes 540672 | tf_op jit(solution)/shard_map/while/body/eval_jaxpr/all_gather | solution.py:11
  1151.9 39.4 %all-gather.3 = f32[256,512]{1,0:T(8,128)S(1)} all-gather(f32[8,512]{1,0:T(8,128)S(1)} %convolution_bitcast_fusion.6), channel_id=2, replica_groups=mesh['row'=8,'col'=4] {'row','col'}, dimensions={0}, use_global_device_ids=true | all-gather | bytes 540672 | tf_op jit(solution)/shard_map/while/body/eval_jaxpr/all_gather | solution.py:11
  1194.9 38.1 %all-gather.3 = f32[256,512]{1,0:T(8,128)S(1)} all-gather(f32[8,512]{1,0:T(8,128)S(1)} %convolution_bitcast_fusion.6), channel_id=2, replica_groups=mesh['row'=8,'col'=4] {'row','col'}, dimensions={0}, use_global_device_ids=true | all-gather | bytes 540672 | tf_op jit(solution)/shard_map/while/body/eval_jaxpr/all_gather | solution.py:11
  1236.6 39.4 %all-gather.3 = f32[256,512]{1,0:T(8,128)S(1)} all-gather(f32[8,512]{1,0:T(8,128)S(1)} %convolution_bitcast_fusion.6), channel_id=2, replica_groups=mesh['row'=8,'col'=4] {'row','col'}, dimensions={0}, use_global_device_ids=true | all-gather | bytes 540672 | tf_op jit(solution)/shard_map/while/body/eval_jaxpr/all_gather | solution.py:11
  1321.3 39.4 %all-gather.3 = f32[256,512]{1,0:T(8,128)S(1)} all-gather(f32[8,512]{1,0:T(8,128)S(1)} %convolution_bitcast_fusion.6), channel_id=2, replica_groups=mesh['row'=8,'col'=4] {'row','col'}, dimensions={0}, use_global_device_ids=true | all-gather | bytes 540672 | tf_op jit(solution)/shard_map/while/body/eval_jaxpr/all_gather | solution.py:11
  (327 shorter events, 214.8 us)
Async XLA Ops:
  0.6 1405.0 %copy-start = (bf16[1,512,512]{2,1,0:T(8,128)(2,1)S(1)}, bf16[1,512,512]{2,1,0:T(8,128)(2,1)}, u32[]{:S(2)}) copy-start(bf16[1,512,512]{2,1,0:T(8,128)(2,1)} %param.20) | copy-start | bytes 1572868
  721.0 684.2 %copy-start.1 = (bf16[1,512,1024]{2,1,0:T(8,128)(2,1)S(1)}, bf16[1,512,1024]{2,1,0:T(8,128)(2,1)}, u32[]{:S(2)}) copy-start(bf16[1,512,1024]{2,1,0:T(8,128)(2,1)} %param.19) | copy-start | bytes 3145732
  721.0 684.6 %copy-start.2 = (bf16[1,8,512]{2,1,0:T(8,128)(2,1)S(1)}, bf16[1,8,512]{2,1,0:T(8,128)(2,1)}, u32[]{:S(2)}) copy-start(bf16[1,8,512]{2,1,0:T(8,128)(2,1)} %param.18) | copy-start | bytes 24580
